TPU v7x, 8 devices: a whole 2x2x1 slice. The times are simulated.
8 devices in a mesh: dp: 2 (over y, z), ep: 4 (over x, core).
Axes of the slice: x: 2, y: 2, z: 1, core: 2. Of those that a mesh axis runs over, the one named last changes fastest.
Arguments:
- x: bfloat16 [2, 4, 256, 7168], P('dp', 'ep'), parts along dimension 0
- expert: int32 [2, 4, 256, 8], P('dp', 'ep'), parts along dimension 0
- slot: int32 [2, 4, 256, 8], P('dp', 'ep'), parts along dimension 0
- gate: float32 [2, 4, 256, 8], P('dp', 'ep'), parts along dimension 0
- w_gate: bfloat16 [32, 7168, 2048], P('ep')
- w_up: bfloat16 [32, 7168, 2048], P('ep')
- w_down: bfloat16 [32, 2048, 7168], P('ep')
- s_gate: bfloat16 [7168, 2048], replicated
- s_up: bfloat16 [7168, 2048], replicated
- s_down: bfloat16 [2048, 7168], replicated
Outputs:
- y: bfloat16 [2, 4, 256, 7168], P('dp', 'ep'), parts along dimension 0
There are 2 independent parts. A program takes and returns all parts, laid end to end along the dimension named above; an argument that names none is the same for every part.
All inputs are finite; a program needn't handle non-finite values.
Results may differ from a plain program's by a relative error of at most 0.009.
Values are sent between devices in bfloat16 or wider.
A program may use at most 2 GiB of HBM per device.

v0:
```python
import jax
import jax.numpy as jnp
from jax import lax
from jax.sharding import NamedSharding, PartitionSpec as P


def einsum(form, a, b):
    return jnp.einsum(form, a.astype(jnp.float32), b.astype(jnp.float32))


def for_all(x, s_gate, s_up, s_down):
    h = jax.nn.silu(einsum("...d,df->...f", x, s_gate)) * einsum("...d,df->...f", x, s_up)
    return einsum("...f,fd->...d", h.astype(jnp.bfloat16), s_down)


def solution(mesh):
    def placed(v, *spec):
        return lax.with_sharding_constraint(v, NamedSharding(mesh, P(*spec)))

    def step(x, expert, slot, gate, w_gate, w_up, w_down, s_gate, s_up, s_down):
        experts, (tokens, top) = w_gate.shape[0], expert.shape[2:]
        slots = 5 * tokens * top // (4 * experts)
        to_expert = jax.nn.one_hot(expert, experts, dtype=jnp.bfloat16)
        to_slot = jax.nn.one_hot(slot, slots, dtype=jnp.bfloat16)
        weighted = to_expert * gate[..., None].astype(jnp.bfloat16)
        dispatch = einsum("abtke,abtkc->abtec", to_expert, to_slot).astype(jnp.bfloat16)
        combine = einsum("abtke,abtkc->abtec", weighted, to_slot).astype(jnp.bfloat16)
        z = einsum("abtec,abtd->aebcd", dispatch, x).astype(jnp.bfloat16)
        z = placed(z, "dp", None, "ep", None, None)
        z = placed(z, "dp", "ep", None, None, None)
        h = jax.nn.silu(einsum("aebcd,edf->aebcf", z, w_gate))
        h = (h * einsum("aebcd,edf->aebcf", z, w_up)).astype(jnp.bfloat16)
        out = einsum("aebcf,efd->aebcd", h, w_down).astype(jnp.bfloat16)
        out = placed(out, "dp", "ep", None, None, None)
        out = placed(out, "dp", None, "ep", None, None)
        y = einsum("abtec,aebcd->abtd", combine, out)
        return (y + for_all(x, s_gate, s_up, s_down)).astype(jnp.bfloat16)

    return step
```

profile of v0, /device:TPU:0, one launch (start us, length us, event | category | flops | bytes accessed | tf_op | source)
XLA Modules:
  0.0 1220.6 jit_solution(1787274517919335552)
XLA Ops:
  0.0 0.8 copy.11
  0.8 0.0 copy-start.1
  0.8 0.8 copy.9
  1.7 0.0 copy-start.3
  1.7 2.6 convolution_convert_fusion.2
  4.3 18.4 %convolution_convert_fusion = bf16[32,80,7168]{2,1,0:T(8,128)(2,1)} fusion(bf16[1,1,256,7168]{3,2,1,0:T(8,128)(2,1)} %param.3, bf16[256,32,80]{2,1,0:T(8,128)(2,1)S(1)} %convolution_convert_fusion.2), kind=kOutput, calls=%fused_computation.11 | convolution fusion | flops 9413591040 | bytes 41680896 | tf_op jit(solution)/abtec,abtd->aebcd/dot_general | solution.py:8
  22.8 0.0 copy-done.1
  22.8 0.0 copy-done.3
  22.8 417.0 %all-to-all.4 = bf16[1,4,8,1,80,7168]{5,4,2,3,0,1:T(8,128)(2,1)} all-to-all(bf16[1,4,8,1,80,7168]{5,4,2,3,0,1:T(8,128)(2,1)} %bitcast.140), channel_id=1, replica_groups=mesh['dp'=2,'ep'=4] {'ep'}, dimensions={1} | all-to-all | bytes 73400320 | tf_op jit(solution)/sharding_constraint;jit(solution)/sharding_constraint | solution.py:18
  439.8 107.2 %fusion.2 = f32[8,4,80,2048]{3,2,1,0:T(8,128)} fusion(bf16[8,7168,2048]{2,1,0:T(8,128)(2,1)} %param.5, bf16[1,4,8,1,80,7168]{5,4,2,3,0,1:T(8,128)(2,1)} %all-to-all.4), kind=kOutput, calls=%fused_computation.2 | convolution fusion | flops 75161927680 | bytes 292552704 | tf_op jit(solution)/aebcd,edf->aebcf/dot_general | solution.py:8
  547.0 103.2 %fusion.80 = bf16[8,4,80,2048]{3,2,1,0:T(8,128)(2,1)} fusion(f32[8,4,80,2048]{3,2,1,0:T(8,128)} %fusion.2, bf16[8,7168,2048]{2,1,0:T(8,128)(2,1)} %param.4, bf16[1,4,8,1,80,7168]{5,4,2,3,0,1:T(8,128)(2,1)} %all-to-all.4), kind=kOutput, calls=%fused_computation.19.clone.1 | convolution fusion | flops 75193384960 | bytes 303038464 | tf_op jit(solution)/aebcd,edf->aebcf/dot_general | solution.py:8
  650.1 98.0 %convert_bitcast_fusion = bf16[1,8,4,1,80,7168]{5,4,2,1,3,0:T(8,128)(2,1)} fusion(bf16[8,2048,7168]{2,1,0:T(8,128)(2,1)} %param.6, bf16[8,4,80,2048]{3,2,1,0:T(8,128)(2,1)} %fusion.80), kind=kOutput, calls=%fused_computation.8 | convolution fusion | flops 75180277760 | bytes 282066944 | tf_op jit(solution)/aebcf,efd->aebcd/dot_general | solution.py:8
  748.1 25.1 %copy.15 = bf16[1,8,4,1,80,7168]{5,4,1,3,0,2:T(8,128)(2,1)} copy(bf16[1,8,4,1,80,7168]{5,4,2,1,3,0:T(8,128)(2,1)} %convert_bitcast_fusion) | data formatting | bytes 73400320 | tf_op jit(solution)/sharding_constraint;jit(solution)/sharding_constraint | solution.py:18
  773.2 0.0 copy-start.4
  773.2 10.7 all-to-all-start.1
  783.9 0.0 copy-done.5
  784.0 0.1 copy.10
  784.1 3.0 convolution_convert_fusion.1
  787.1 0.0 copy-start
  787.2 14.5 %fusion.39 = f32[1,1,256,2048]{3,2,1,0:T(8,128)S(1)} fusion(bf16[7168,2048]{1,0:T(8,128)(2,1)} %param.7, bf16[1,1,256,7168]{3,2,1,0:T(8,128)(2,1)} %param.3), kind=kOutput, calls=%fused_computation.31 | convolution fusion | flops 7516192768 | bytes 35127296 | tf_op jit(solution)/...d,df->...f/dot_general | solution.py:8
  801.7 13.9 %fusion.45 = bf16[256,2048]{1,0:T(8,128)(2,1)S(1)} fusion(bf16[7168,2048]{1,0:T(8,128)(2,1)} %param.8, bf16[1,1,256,7168]{3,2,1,0:T(8,128)(2,1)S(1)} %copy-done, f32[1,1,256,2048]{3,2,1,0:T(8,128)S(1)} %fusion.39), kind=kOutput, calls=%fused_computation.33 | convolution fusion | flops 7519338496 | bytes 36175872 | tf_op jit(solution)/...d,df->...f/dot_general | solution.py:8
  815.6 364.2 %all-to-all-done.1 = bf16[1,8,4,1,80,7168]{5,4,1,3,0,2:T(8,128)(2,1)} async-done(((bf16[1,8,4,1,80,7168]{5,4,1,3,0,2:T(8,128)(2,1)}), bf16[1,8,4,1,80,7168]{5,4,1,3,0,2:T(8,128)(2,1)}, u32[]{:S(2)}, u32[]{:S(2)}) %all-to-all-start.1) | async-done | bytes 36700192 | tf_op jit(solution)/sharding_constraint;jit(solution)/sharding_constraint | solution.py:18
  1179.9 21.0 %convolution_bitcast_fusion = f32[256,7168]{1,0:T(8,128)} fusion(bf16[32,80,7168]{2,1,0:T(8,128)(2,1)} %bitcast.25, bf16[256,32,80]{2,1,0:T(8,128)(2,1)S(1)} %convolution_convert_fusion.1), kind=kOutput, calls=%fused_computation.20 | convolution fusion | flops 9395240960 | bytes 45350912 | tf_op jit(solution)/abtec,aebcd->abtd/dot_general | solution.py:8
  1200.8 19.7 %fusion.27 = bf16[1,1,256,7168]{3,2,1,0:T(8,128)(2,1)} fusion(f32[256,7168]{1,0:T(8,128)} %convolution_bitcast_fusion, bf16[256,2048]{1,0:T(8,128)(2,1)S(1)} %fusion.45, bf16[2048,7168]{1,0:T(8,128)(2,1)} %param.9), kind=kOutput, calls=%fused_computation.23 | convolution fusion | flops 7519862784 | bytes 41418752 | tf_op jit(solution)/...f,fd->...d/dot_general | solution.py:8
  (6 shorter events, 0.0 us)
Async XLA Ops:
  0.8 22.0 %copy-start.1 = (s32[256,8]{1,0:T(8,128)}, s32[256,8]{1,0:T(8,128)S(1)}, u32[]{:S(2)}) copy-start(s32[256,8]{1,0:T(8,128)S(1)} %copy.11) | copy-start | bytes 24580
  1.7 21.1 %copy-start.3 = (s32[256,8]{1,0:T(8,128)}, s32[256,8]{1,0:T(8,128)S(1)}, u32[]{:S(2)}) copy-start(s32[256,8]{1,0:T(8,128)S(1)} %copy.9) | copy-start | bytes 24580
  773.2 10.8 copy-start.5
  773.2 10.9 copy-start.2
  773.2 10.9 copy-start.4
  773.2 406.7 %all-to-all-start.1 = ((bf16[1,8,4,1,80,7168]{5,4,1,3,0,2:T(8,128)(2,1)}), bf16[1,8,4,1,80,7168]{5,4,1,3,0,2:T(8,128)(2,1)}, u32[]{:S(2)}, u32[]{:S(2)}) async-start(bf16[1,8,4,1,80,7168]{5,4,1,3,0,2:T(8,128)(2,1)} %copy.15), calls=%async_computation.1 | async-start | bytes 73400320 | tf_op jit(solution)/sharding_constraint;jit(solution)/sharding_constraint | solution.py:18
  787.1 14.5 %copy-start = (bf16[1,1,256,7168]{3,2,1,0:T(8,128)(2,1)S(1)}, bf16[1,1,256,7168]{3,2,1,0:T(8,128)(2,1)}, u32[]{:S(2)}) copy-start(bf16[1,1,256,7168]{3,2,1,0:T(8,128)(2,1)} %param.3) | copy-start | bytes 11010052
where the time goes:
time: 1220 us
  blocking collectives  417 us (34%)
  matrix products  402 us (33%)
  waiting for transfers between devices  364 us (30%)
  local copies, waits for them, and re-layouts  26.9 us (2%)
    another operation x1, blocking collectives, placed(): return lax.with_sharding_constraint(v, NamedSharding(mesh, P(*spec)))  417 us
    dot_general x10, matrix products, einsum(): return jnp.einsum(form, a.astype(jnp.float32), b.astype(jnp.float32))  402 us
    another operation x1, waiting for transfers between devices, placed(): return lax.with_sharding_constraint(v, NamedSharding(mesh, P(*spec)))  364 us
    another operation x1, local copies, waits for them, and re-layouts, placed(): return lax.with_sharding_constraint(v, NamedSharding(mesh, P(*spec)))  25.1 us
  transfers between devices with their start and end apart: 1, of which 1 were waited for; matrix products, arithmetic and copies ran while one was open for 3% of the time, Pallas kernels for 0%

commit v1 on v0

v1 whole, which is shorter than its diff:
```python
import functools

import jax
import jax.numpy as jnp
from jax import lax
from jax.experimental import pallas as pl
from jax.experimental.pallas import tpu as pltpu
from jax.sharding import PartitionSpec as P

HALF = 160
SEG = 80
MESH = pl.DeviceIdType.MESH
F32, BF16 = jnp.float32, jnp.bfloat16
ANY = pl.BlockSpec(memory_space=pl.ANY)
VMEM = pl.BlockSpec(memory_space=pltpu.VMEM)
SMEM = pl.BlockSpec(memory_space=pltpu.SMEM)


def offsets(npad, e):
    offs, total = [], 0
    for k in range(4):
        offs.append(total)
        total = total + npad[k, e]
    return offs, total


def up_kernel(tile, depth, npad, st, x0, x1, x2, x3, wg, wu, h, xv, z, wbuf, hbuf, hout, xsem, wsem, hsem):
    experts, rows, ff = wg.shape
    per = ff // tile
    steps = experts * per

    def weights(i):
        e, cols, s = i // per, pl.ds(pl.multiple_of((i % per) * tile, tile), tile), i % depth
        return [
            pltpu.make_async_copy(w.at[e, :, cols], wbuf.at[s, :, pl.ds(n * tile, tile)], wsem.at[s, n])
            for n, w in enumerate((wg, wu))
        ]

    def result(e):
        return pltpu.make_async_copy(hout.at[e % 2], h.at[e], hsem.at[e % 2])

    blocks = [pltpu.make_async_copy(x, xv.at[k], xsem.at[k]) for k, x in enumerate((x0, x1, x2, x3))]
    for c in blocks:
        c.start()
    for i in range(depth):
        for c in weights(i):
            c.start()
    for c in blocks:
        c.wait()

    def dispatch(e):
        offs, _ = offsets(npad, e)
        line = lax.broadcasted_iota(jnp.int32, (SEG, xv.shape[1]), 0)
        for k in range(4):
            pick = jnp.where(line == st[k, e], 1.0, 0.0).astype(BF16)
            at = pl.ds(pl.multiple_of(offs[k], 16), SEG)
            z[at, :] = jnp.dot(pick, xv[k], preferred_element_type=F32).astype(BF16)

    def step(i, _):
        e, j, s = i // per, i % per, i % depth
        offs, total = offsets(npad, e)

        @pl.when(j == 0)
        def _():
            dispatch(e)

        for c in weights(i):
            c.wait()

        def work(n):
            gu = jnp.dot(z[:n, :], wbuf[s], preferred_element_type=F32)
            g, u = gu[:, :tile], gu[:, tile:]
            hbuf[:n, pl.ds(pl.multiple_of(j * tile, tile), tile)] = (jax.nn.silu(g) * u).astype(BF16)

        @pl.when((total > 0) & (total <= HALF))
        def _():
            work(HALF)

        @pl.when(total > HALF)
        def _():
            work(2 * HALF)

        @pl.when(i + depth < steps)
        def _():
            for c in weights(i + depth):
                c.start()

        @pl.when(j == per - 1)
        def _():
            @pl.when(e >= 2)
            def _():
                result(e).wait()

            line = lax.broadcasted_iota(jnp.int32, (SEG, ff), 0)
            for k in range(4):
                part = hbuf[pl.ds(pl.multiple_of(offs[k], 16), SEG), :]
                hout[e % 2, SEG * k : SEG * (k + 1), :] = jnp.where(line < npad[k, e], part, jnp.zeros_like(part))
            result(e).start()

        return 0

    lax.fori_loop(0, steps, step, 0)
    for e in (experts - 2, experts - 1):
        result(e).wait()


def up_call(npad, st, xs, wg, wu):
    experts, rows, ff = wg.shape
    tile, depth = 256, 4
    tokens = xs[0].shape[0]
    return pl.pallas_call(
        functools.partial(up_kernel, tile, depth),
        out_shape=jax.ShapeDtypeStruct((experts, 2 * HALF, ff), BF16),
        in_specs=[SMEM, VMEM] + [ANY] * 6,
        out_specs=ANY,
        scratch_shapes=[
            pltpu.VMEM((4, tokens, rows), BF16),
            pltpu.VMEM((2 * HALF, rows), BF16),
            pltpu.VMEM((depth, rows, 2 * tile), BF16),
            pltpu.VMEM((2 * HALF, ff), BF16),
            pltpu.VMEM((2, 2 * HALF, ff), BF16),
            pltpu.SemaphoreType.DMA((4,)),
            pltpu.SemaphoreType.DMA((depth, 2)),
            pltpu.SemaphoreType.DMA((2,)),
        ],
        compiler_params=pltpu.CompilerParams(vmem_limit_bytes=60 * 2**20),
        cost_estimate=pl.CostEstimate(
            flops=2 * experts * HALF * rows * ff * 2, bytes_accessed=experts * rows * ff * 4, transcendentals=0
        ),
        name="up",
    )(npad, st, *xs, wg, wu)


def down_kernel(tiles, tile, depth, sc, gc, h, wd, shared, y, hv, wbuf, rows, mix, own, far32, outs, lands, sbuf, ybuf, hsem, wsem, ssem, ysem, send, recv):
    experts, ff, _ = wd.shape
    steps = tiles * experts
    tokens, room = mix.shape[1:]
    me = lax.axis_index("ep")
    near, far = me + 1 - 2 * (me % 2), (me + 2) % 4

    barrier = pltpu.get_barrier_semaphore()
    for d in (near, far):
        pl.semaphore_signal(barrier, inc=1, device_id={"ep": d}, device_id_type=MESH)

    def columns(t):
        return pl.ds(pl.multiple_of(t * tile, tile), tile)

    def weights(i):
        s = i % depth
        return pltpu.make_async_copy(wd.at[i % experts, :, columns(i // experts)], wbuf.at[s], wsem.at[s])

    def addend(t):
        return pltpu.make_async_copy(shared.at[:, columns(t)], sbuf.at[t % 2], ssem.at[t % 2])

    def result(t):
        return pltpu.make_async_copy(ybuf.at[t % 2], y.at[:, columns(t)], ysem.at[t % 2])

    def sending(kind, t):
        return pltpu.make_async_remote_copy(
            src_ref=outs.at[kind, t % 2],
            dst_ref=lands.at[kind, t],
            send_sem=send.at[kind, t],
            recv_sem=recv.at[kind, t],
            device_id={"ep": far if kind == 2 else near},
            device_id_type=MESH,
        )

    loads = [pltpu.make_async_copy(h.at[e], hv.at[e], hsem.at[e]) for e in range(experts)]
    loads[0].start()
    weights(0).start()
    for c in loads[1:]:
        c.start()
    for i in range(1, depth):
        weights(i).start()
    for t in range(2):
        addend(t).start()
    place = lax.broadcasted_iota(jnp.int32, (tokens, room), 1)
    for k in range(4):
        m = jnp.zeros((tokens, room), F32)
        for e in range(experts):
            s = sc[k, :, e : e + 1]
            s = jnp.where(s >= 0, s + SEG * e, -1)
            m = jnp.where(place == s, gc[k, :, e : e + 1], m)
        mix[k] = m.astype(BF16)
    pl.semaphore_wait(barrier, 2)
    for c in loads:
        c.wait()

    def combine(t):
        @pl.when(t >= 2)
        def _():
            sending(0, t - 2).wait_send()
            sending(1, t - 2).wait_send()

        outs[0, t % 2] = jnp.dot(mix[1], rows[1], preferred_element_type=F32).astype(BF16)
        outs[1, t % 2] = jnp.dot(mix[3], rows[3], preferred_element_type=F32).astype(BF16)
        far32[t % 2] = jnp.dot(mix[2], rows[2], preferred_element_type=F32)
        own[t % 4] = jnp.dot(mix[0], rows[0], preferred_element_type=F32)
        sending(1, t).start()
        sending(0, t).start()

    def forward(t):
        sending(1, t).wait_recv()

        @pl.when(t >= 2)
        def _():
            sending(2, t - 2).wait_send()

        outs[2, t % 2] = (far32[t % 2] + lands[1, t].astype(F32)).astype(BF16)
        sending(2, t).start()

    def final(t):
        sending(0, t).wait_recv()
        sending(2, t).wait_recv()
        addend(t).wait()

        @pl.when(t >= 2)
        def _():
            result(t - 2).wait()

        ybuf[t % 2] = (own[t % 4] + sbuf[t % 2] + lands[0, t].astype(F32) + lands[2, t].astype(F32)).astype(BF16)
        result(t).start()

        @pl.when(t + 2 < tiles)
        def _():
            addend(t + 2).start()

    def step(i, _):
        t, e, s = i // experts, i % experts, i % depth
        weights(i).wait()
        o = jnp.dot(hv[e], wbuf[s], preferred_element_type=F32).astype(BF16)
        for k in range(4):
            rows[k, pl.ds(pl.multiple_of(e * SEG, 16), SEG), :] = o[SEG * k : SEG * (k + 1)]

        @pl.when(i + depth < steps)
        def _():
            weights(i + depth).start()

        @pl.when((e == 1) & (t >= 1))
        def _():
            forward(t - 1)

        @pl.when((e == 5) & (t >= 2))
        def _():
            final(t - 2)

        @pl.when(e == experts - 1)
        def _():
            combine(t)

        return 0

    lax.fori_loop(0, steps, step, 0)
    last = jnp.int32(tiles - 1)
    forward(last)
    final(last - 1)
    final(last)
    for t in (tiles - 2, tiles - 1):
        result(t).wait()
        for kind in range(3):
            sending(kind, t).wait_send()


def down_call(sc, gc, h, wd, shared):
    experts, ff, width = wd.shape
    tile, depth = 1024, 3
    tiles = width // tile
    tokens = sc.shape[1]
    room = SEG * experts
    return pl.pallas_call(
        functools.partial(down_kernel, tiles, tile, depth),
        out_shape=jax.ShapeDtypeStruct((tokens, width), BF16),
        in_specs=[VMEM, VMEM, ANY, ANY, ANY],
        out_specs=ANY,
        scratch_shapes=[
            pltpu.VMEM((experts, 4 * SEG, ff), BF16),
            pltpu.VMEM((depth, ff, tile), BF16),
            pltpu.VMEM((4, room, tile), BF16),
            pltpu.VMEM((4, tokens, room), BF16),
            pltpu.VMEM((4, tokens, tile), F32),
            pltpu.VMEM((2, tokens, tile), F32),
            pltpu.VMEM((3, 2, tokens, tile), BF16),
            pltpu.VMEM((3, tiles, tokens, tile), BF16),
            pltpu.VMEM((2, tokens, tile), F32),
            pltpu.VMEM((2, tokens, tile), BF16),
            pltpu.SemaphoreType.DMA((experts,)),
            pltpu.SemaphoreType.DMA((depth,)),
            pltpu.SemaphoreType.DMA((2,)),
            pltpu.SemaphoreType.DMA((2,)),
            pltpu.SemaphoreType.DMA((3, tiles)),
            pltpu.SemaphoreType.DMA((3, tiles)),
        ],
        compiler_params=pltpu.CompilerParams(vmem_limit_bytes=63 * 2**20, collective_id=0, has_side_effects=True),
        cost_estimate=pl.CostEstimate(
            flops=2 * experts * 4 * SEG * width * ff, bytes_accessed=experts * width * ff * 2, transcendentals=0
        ),
        name="down",
    )(sc, gc, h, wd, shared)


def solution(mesh):
    members = mesh.shape["ep"]

    def move(v, hop):
        return lax.ppermute(v, "ep", [(i, i ^ hop) for i in range(members)])

    def body(x, expert, slot, gate, wg, wu, wd, sg, su, sd):
        x, expert, slot, gate = (v[0, 0] for v in (x, expert, slot, gate))
        local = wg.shape[0]
        me = lax.axis_index("ep")
        far_x = move(x, 2)
        near_x = move(x, 1)

        hit = (expert[:, :, None] == jnp.arange(local * members)) & (slot < SEG)[:, :, None]
        slots = jnp.max(jnp.where(hit, slot[:, :, None], -1), axis=1)
        gates = jnp.sum(jnp.where(hit, gate.astype(BF16).astype(F32)[:, :, None], 0.0), axis=1)
        table = jnp.stack([slots.astype(F32), gates])
        parts = []
        for hop in range(members):
            part = lax.dynamic_slice_in_dim(table, (me ^ hop) * local, local, axis=2)
            parts.append(move(part, hop) if hop else part)
        table = jnp.stack(parts)
        sc, gc = table[:, 0].astype(jnp.int32), table[:, 1]
        npad = (jnp.max(sc, axis=1) + 16) // 16 * 16
        st = jnp.swapaxes(sc, 1, 2)[:, :, None, :]

        g = jnp.dot(x, sg, preferred_element_type=F32)
        u = jnp.dot(x, su, preferred_element_type=F32)
        shared = jnp.dot((jax.nn.silu(g) * u).astype(BF16), sd, preferred_element_type=F32)

        shared, far_x = lax.optimization_barrier((shared, far_x))
        diag_x = move(far_x, 1)
        h = up_call(npad, st, (x, near_x, far_x, diag_x), wg, wu)

        return down_call(sc, gc, h, wd, shared)[None, None]

    tok, exp, whole = P("dp", "ep", None, None), P("ep", None, None), P(None, None)
    return jax.shard_map(
        body,
        mesh=mesh,
        in_specs=(tok, tok, tok, tok, exp, exp, exp, whole, whole, whole),
        out_specs=tok,
        check_vma=False,
    )
```

time: 1220 us -> 398 us (0.33)
  the two profiles are of different devices: /device:TPU:0 before, /device:TPU:6 now
where the time goes in v1:
time: 398 us; the launch traced here: 406 us
  Pallas kernels  311 us (78%)
  waiting for transfers between devices  43.2 us (11%)
  matrix products  41.6 us (10%)
  local copies, waits for them, and re-layouts  6.1 us (2%)
    pallas_call x1, Pallas kernels, up_call(): pl.pallas_call(functools.partial(up_kernel, tile, depth), out_shape=jax.S...  156 us
    pallas_call x1, Pallas kernels, down_call(): pl.pallas_call(functools.partial(down_kernel, tiles, tile, depth), out_sh...  155 us
    ppermute x6, waiting for transfers between devices, move(): return lax.ppermute(v, 'ep', [(i, i ^ hop) for i in range(members)])  43.2 us
    dot_general x1, matrix products, body(): jnp.dot((jax.nn.silu(g) * u).astype(BF16), sd, preferred_element_type=F32)  27.2 us
    dot_general x1, matrix products, body(): g = jnp.dot(x, sg, preferred_element_type=F32)  14.5 us
  transfers between devices with their start and end apart: 6, of which 2 were waited for; matrix products, arithmetic and copies ran while one was open for 11% of the time, Pallas kernels for 0%

profile of v1, /device:TPU:6, one launch (start us, length us, event | category | flops | bytes accessed | tf_op | source)
XLA Modules:
  0.0 405.8 jit_solution(3768470094785298343)
XLA Ops:
  0.0 0.5 collective-permute-start.4
  0.5 0.0 collective-permute-start.3
  0.5 14.5 %fusion.19 = f32[256,2048]{1,0:T(8,128)S(1)} fusion(bf16[7168,2048]{1,0:T(8,128)(2,1)} %param.17, bf16[1,1,256,7168]{3,2,1,0:T(8,128)(2,1)} %param.10), kind=kOutput, calls=%fused_computation.42 | convolution fusion | flops 7516192768 | bytes 35127296 | tf_op jit(solution)/shard_map/dot_general | solution.py:327
  15.0 0.0 copy-start
  15.0 0.0 copy-start.1
  15.0 0.0 copy-start.2
  15.1 27.2 %fusion.1.shared = f32[256,7168]{1,0:T(8,128)} fusion(bf16[2048,7168]{1,0:T(8,128)(2,1)} %param.19, bf16[7168,2048]{1,0:T(8,128)(2,1)} %param.18, f32[256,2048]{1,0:T(8,128)S(1)} %fusion.19, bf16[1,1,256,7168]{3,2,1,0:T(8,128)(2,1)} %param.10), kind=kOutput, calls=%fused_computation.2 | convolution fusion | flops 15035531264 | bytes 71827456 | tf_op jit(solution)/shard_map/dot_general | solution.py:329
  42.2 38.9 %collective-permute-done.4.x2 = bf16[256,7168]{1,0:T(8,128)(2,1)} collective-permute-done((bf16[256,7168]{1,0:T(8,128)(2,1)}, bf16[256,7168]{1,0:T(8,128)(2,1)}, u32[]{:S(2)}, u32[]{:S(2)}) %collective-permute-start.4) | collective-permute-done | bytes 3670048 | tf_op jit(solution)/shard_map/ppermute | solution.py:305
  81.1 0.0 collective-permute-start.5
  81.1 0.1 select_reduce_fusion.1
  81.2 0.1 select_reduce_fusion
  81.3 0.5 collective-permute-start
  81.8 0.5 collective-permute-start.1
  82.4 0.8 collective-permute-start.2
  83.2 4.3 %collective-permute-done = f32[2,256,8]{1,2,0:T(8,128)S(1)} collective-permute-done((f32[2,256,8]{1,2,0:T(8,128)S(1)}, f32[2,256,8]{1,2,0:T(8,128)S(1)}, u32[]{:S(2)}, u32[]{:S(2)}) %collective-permute-start) | collective-permute-done | bytes 16416 | tf_op jit(solution)/shard_map/ppermute | solution.py:305
  87.5 0.2 copy.25
  87.7 0.9 convert_bitcast_fusion
  88.6 0.8 copy.27.st
  89.4 1.0 copy.28
  90.4 0.1 convert_reduce_fusion
  90.5 0.6 fusion.15.npad
  91.1 155.8 %up.1.h = bf16[8,320,2048]{2,1,0:T(8,128)(2,1)} custom-call(s32[4,8]{1,0:T(4,128)} %fusion.15.npad, s32[4,8,1,256]{3,2,1,0:T(1,128)} %copy.27.st, bf16[256,7168]{1,0:T(8,128)(2,1)} %bitcast.34, bf16[256,7168]{1,0:T(8,128)(2,1)} %collective-permute-done.3.x1, bf16[256,7168]{1,0:T(8,128)(2,1)} %collective-permute-done.4.x2, ...), custom_call_target="tpu_custom_call" | custom-call | flops 75161927680 | bytes 469762048 | tf_op jit(solution)/shard_map/up/pallas_call | solution.py:111
  246.9 154.8 %down.1 = bf16[256,7168]{1,0:T(8,128)(2,1)} custom-call(s32[4,256,8]{2,1,0:T(8,128)} %get-tuple-element.10.sc, f32[4,256,8]{2,1,0:T(8,128)} %bitcast.36, bf16[8,320,2048]{2,1,0:T(8,128)(2,1)} %up.1.h, bf16[8,2048,7168]{2,1,0:T(8,128)(2,1)} %wd.1, f32[256,7168]{1,0:T(8,128)} %fusion.1.shared), custom_call_target="tpu_custom_call" | custom-call | flops 75161927680 | bytes 234881024 | tf_op jit(solution)/shard_map/down/pallas_call | solution.py:270
  401.7 4.1 %copy.30 = bf16[1,1,256,7168]{3,2,1,0:T(8,128)(2,1)} copy(bf16[1,1,256,7168]{3,2,1,0:T(8,128)(2,1)} %bitcast.35) | data formatting | bytes 7340032
  (13 shorter events, 0.1 us)
Async XLA Ops:
  0.0 81.1 %collective-permute-start.4 = (bf16[256,7168]{1,0:T(8,128)(2,1)}, bf16[256,7168]{1,0:T(8,128)(2,1)}, u32[]{:S(2)}, u32[]{:S(2)}) collective-permute-start(bf16[256,7168]{1,0:T(8,128)(2,1)} %bitcast.32), channel_id=1, source_target_pairs={{0,2},{1,3},{2,0},{3,1},{4,6},{5,7},{6,4},{7,5}} | collective-permute-start | bytes 11010056 | tf_op jit(solution)/shard_map/ppermute | solution.py:305
  0.5 90.5 %collective-permute-start.3 = (bf16[256,7168]{1,0:T(8,128)(2,1)}, bf16[256,7168]{1,0:T(8,128)(2,1)}, u32[]{:S(2)}, u32[]{:S(2)}) collective-permute-start(bf16[256,7168]{1,0:T(8,128)(2,1)} %bitcast.33), channel_id=1, source_target_pairs={{0,1},{1,0},{2,3},{3,2},{4,5},{5,4},{6,7},{7,6}} | collective-permute-start | bytes 11010056 | tf_op jit(solution)/shard_map/ppermute | solution.py:305
  15.0 66.1 %copy-start = (s32[1,1,256,8]{2,3,1,0:T(8,128)S(1)}, s32[1,1,256,8]{2,3,1,0:T(8,128)}, u32[]{:S(2)}) copy-start(s32[1,1,256,8]{2,3,1,0:T(8,128)} %param.12) | copy-start | bytes 24580
  15.0 66.1 %copy-start.1 = (s32[1,1,256,8]{2,3,1,0:T(8,128)S(1)}, s32[1,1,256,8]{2,3,1,0:T(8,128)}, u32[]{:S(2)}) copy-start(s32[1,1,256,8]{2,3,1,0:T(8,128)} %param.11) | copy-start | bytes 24580
  15.0 66.1 %copy-start.2 = (f32[1,1,256,8]{2,3,1,0:T(8,128)S(1)}, f32[1,1,256,8]{2,3,1,0:T(8,128)}, u32[]{:S(2)}) copy-start(f32[1,1,256,8]{2,3,1,0:T(8,128)} %param.13) | copy-start | bytes 24580
  81.1 10.0 %collective-permute-start.5 = (bf16[256,7168]{1,0:T(8,128)(2,1)}, bf16[256,7168]{1,0:T(8,128)(2,1)}, u32[]{:S(2)}, u32[]{:S(2)}) collective-permute-start(bf16[256,7168]{1,0:T(8,128)(2,1)} %collective-permute-done.4.x2), channel_id=1, source_target_pairs={{0,1},{1,0},{2,3},{3,2},{4,5},{5,4},{6,7},{7,6}} | collective-permute-start | bytes 11010056 | tf_op jit(solution)/shard_map/ppermute | solution.py:305
  81.3 6.2 %collective-permute-start = (f32[2,256,8]{1,2,0:T(8,128)S(1)}, f32[2,256,8]{1,2,0:T(8,128)S(1)}, u32[]{:S(2)}, u32[]{:S(2)}) collective-permute-start(f32[2,256,8]{1,2,0:T(8,128)S(1)} %get-tuple-element.14), channel_id=1, source_target_pairs={{0,1},{1,0},{2,3},{3,2},{4,5},{5,4},{6,7},{7,6}} | collective-permute-start | bytes 49160 | tf_op jit(solution)/shard_map/ppermute | solution.py:305
  81.8 5.7 %collective-permute-start.1 = (f32[2,256,8]{1,2,0:T(8,128)S(1)}, f32[2,256,8]{1,2,0:T(8,128)S(1)}, u32[]{:S(2)}, u32[]{:S(2)}) collective-permute-start(f32[2,256,8]{1,2,0:T(8,128)S(1)} %get-tuple-element.15), channel_id=1, source_target_pairs={{0,2},{1,3},{2,0},{3,1},{4,6},{5,7},{6,4},{7,5}} | collective-permute-start | bytes 49160 | tf_op jit(solution)/shard_map/ppermute | solution.py:305
  82.4 5.2 %collective-permute-start.2 = (f32[2,256,8]{1,2,0:T(8,128)S(1)}, f32[2,256,8]{1,2,0:T(8,128)S(1)}, u32[]{:S(2)}, u32[]{:S(2)}) collective-permute-start(f32[2,256,8]{1,2,0:T(8,128)S(1)} %get-tuple-element.16), channel_id=1, source_target_pairs={{0,3},{1,2},{2,1},{3,0},{4,7},{5,6},{6,5},{7,4}} | collective-permute-start | bytes 49160 | tf_op jit(solution)/shard_map/ppermute | solution.py:305

commit v2 on v1

v2 whole, which is shorter than its diff:
```python
import functools

import jax
import jax.numpy as jnp
from jax import lax
from jax.experimental import pallas as pl
from jax.experimental.pallas import tpu as pltpu
from jax.sharding import PartitionSpec as P


FIRST = 2304
UNIT = 256
HALF = 160
SEG = 80
MESH = pl.DeviceIdType.MESH
F32, BF16 = jnp.float32, jnp.bfloat16
ANY = pl.BlockSpec(memory_space=pl.ANY)
VMEM = pl.BlockSpec(memory_space=pltpu.VMEM)
SMEM = pl.BlockSpec(memory_space=pltpu.SMEM)


def offsets(npad, e):
    offs, total = [], 0
    for k in range(4):
        offs.append(total)
        total = total + npad[k, e]
    return offs, total


def up_kernel(first, tile, depth, npad, table, x0, x1, x2, x3, wg, wu, *refs):
    (sums, h, xv, z, wbuf, abuf, hbuf, hout, xsem, wsem, asem, hsem), begins = refs, first == 0
    experts, ff, rows = wg.shape[0], wg.shape[2], z.shape[1]
    per = ff // tile
    steps = experts * per
    units = tile // UNIT
    ring = abuf.shape[0]

    def weights(i):
        e, cols, s = i // per, pl.ds(pl.multiple_of((i % per) * tile, tile), tile), i % depth
        return [
            pltpu.make_async_copy(
                w.at[e, pl.ds(first, rows), cols], wbuf.at[s, :, pl.ds(n * tile, tile)], wsem.at[s, n]
            )
            for n, w in enumerate((wg, wu))
        ]

    def partial(i, act):
        e, j, s = i // per, i % per, i % ring
        _, total = offsets(npad, e)
        for b in range(4):
            band = pl.ds(b * SEG, SEG)
            near, away = abuf.at[s, :, band], sums.at[e, pl.ds(j * units, units), band]

            @pl.when(total > b * SEG)
            def _():
                act(pltpu.make_async_copy(*((near, away) if begins else (away, near)), asem.at[s, b]))

    def result(e):
        return pltpu.make_async_copy(hout.at[e % 2], h.at[e], hsem.at[e % 2])

    def ask(i):
        for c in weights(i):
            c.start()
        if not begins:
            partial(i, lambda c: c.start())

    blocks = []
    for k, x in enumerate((x0, x1, x2, x3)):
        part = x if x.shape[1] == rows else x.at[:, pl.ds(first, rows)]
        blocks.append(pltpu.make_async_copy(part, xv.at[k], xsem.at[k]))
    for c in blocks:
        c.start()
    for i in range(depth):
        ask(i)
    for c in blocks:
        c.wait()

    def dispatch(e):
        offs, _ = offsets(npad, e)
        line = lax.broadcasted_iota(jnp.int32, (SEG, xv.shape[1]), 0).astype(F32)
        for k in range(4):
            pick = jnp.where(line == table[k, 0, pl.ds(e, 1), :], 1.0, 0.0).astype(BF16)
            at = pl.ds(pl.multiple_of(offs[k], 16), SEG)
            z[at, :] = jnp.dot(pick, xv[k], preferred_element_type=F32).astype(BF16)

    def step(i, _):
        e, j, s, a = i // per, i % per, i % depth, i % ring
        offs, total = offsets(npad, e)

        @pl.when(j == 0)
        def _():
            dispatch(e)

        for c in weights(i):
            c.wait()
        if begins:

            @pl.when(i >= ring)
            def _():
                partial(i - ring, lambda c: c.wait())
        else:
            partial(i, lambda c: c.wait())

        def work(n):
            gu = jnp.dot(z[:n, :], wbuf[s], preferred_element_type=F32)
            for v in range(units):
                g, u = (gu[:, m * tile + v * UNIT :][:, :UNIT] for m in range(2))
                if begins:
                    abuf[a, v, :n, :UNIT] = g
                    abuf[a, v, :n, UNIT:] = u
                else:
                    g, u = g + abuf[a, v, :n, :UNIT], u + abuf[a, v, :n, UNIT:]
                    cols = pl.ds(pl.multiple_of(j * tile + v * UNIT, UNIT), UNIT)
                    hbuf[:n, cols] = (jax.nn.silu(g) * u).astype(BF16)

        @pl.when((total > 0) & (total <= HALF))
        def _():
            work(HALF)

        @pl.when(total > HALF)
        def _():
            work(2 * HALF)

        @pl.when(i + depth < steps)
        def _():
            ask(i + depth)

        if begins:
            partial(i, lambda c: c.start())
            return 0

        @pl.when(j == per - 1)
        def _():
            @pl.when(e >= 2)
            def _():
                result(e).wait()

            line = lax.broadcasted_iota(jnp.int32, (SEG, ff), 0)
            for k in range(4):
                part = hbuf[pl.ds(pl.multiple_of(offs[k], 16), SEG), :]
                hout[e % 2, SEG * k : SEG * (k + 1), :] = jnp.where(line < npad[k, e], part, jnp.zeros_like(part))
            result(e).start()

        return 0

    lax.fori_loop(0, steps, step, 0)
    if begins:
        for i in range(steps - ring, steps):
            partial(jnp.int32(i), lambda c: c.wait())
    else:
        for e in (experts - 2, experts - 1):
            result(e).wait()


def begin_kernel(tile, depth, npad, table, x0, x1, x2, x3, wg, wu, sums, xv, z, wbuf, abuf, xsem, wsem, asem):
    refs = (sums, None, xv, z, wbuf, abuf, None, None, xsem, wsem, asem, None)
    up_kernel(0, tile, depth, npad, table, x0, x1, x2, x3, wg, wu, *refs)


def up_call(first, rows, npad, table, xs, wg, wu, sums=None):
    experts, _, ff = wg.shape
    tile, depth = (512, 4) if first == 0 else (512, 3)
    ring, units = (2 if first == 0 else depth), tile // UNIT
    tokens = xs[0].shape[0]
    scratch = [
        pltpu.VMEM((4, tokens, rows), BF16),
        pltpu.VMEM((2 * HALF, rows), BF16),
        pltpu.VMEM((depth, rows, 2 * tile), BF16),
        pltpu.VMEM((ring, units, 2 * HALF, 2 * UNIT), F32),
    ]
    semaphores = [
        pltpu.SemaphoreType.DMA((4,)),
        pltpu.SemaphoreType.DMA((depth, 2)),
        pltpu.SemaphoreType.DMA((ring, 4)),
    ]
    common = dict(
        compiler_params=pltpu.CompilerParams(vmem_limit_bytes=63 * 2**20),
        cost_estimate=pl.CostEstimate(
            flops=2 * experts * HALF * rows * ff * 2, bytes_accessed=experts * rows * ff * 4, transcendentals=0
        ),
    )
    if first == 0:
        return pl.pallas_call(
            functools.partial(begin_kernel, tile, depth),
            out_shape=jax.ShapeDtypeStruct((experts, ff // UNIT, 2 * HALF, 2 * UNIT), F32),
            in_specs=[SMEM, VMEM] + [ANY] * 6,
            out_specs=ANY,
            scratch_shapes=scratch + semaphores,
            name="up_first",
            **common,
        )(npad, table, *xs, wg, wu)
    return pl.pallas_call(
        functools.partial(up_kernel, first, tile, depth),
        out_shape=jax.ShapeDtypeStruct((experts, 2 * HALF, ff), BF16),
        in_specs=[SMEM, VMEM] + [ANY] * 7,
        out_specs=ANY,
        scratch_shapes=scratch
        + [pltpu.VMEM((2 * HALF, ff), BF16), pltpu.VMEM((2, 2 * HALF, ff), BF16)]
        + semaphores
        + [pltpu.SemaphoreType.DMA((2,))],
        name="up_rest",
        **common,
    )(npad, table, *xs, wg, wu, sums)


def shared_kernel(tile, wide, depth, x, sg, su, sd, y, rest, xv, wbuf, dbuf, hbuf, ybuf, xsem, wsem, dsem, ysem):
    ff, width = sd.shape
    ups, downs = ff // tile, width // wide

    def block(n, size):
        return pl.ds(pl.multiple_of(n * size, size), size)

    def up(i):
        return [
            pltpu.make_async_copy(
                w.at[:, block(i, tile)], wbuf.at[i % depth, :, pl.ds(n * tile, tile)], wsem.at[i % depth, n]
            )
            for n, w in enumerate((sg, su))
        ]

    def down(t):
        return pltpu.make_async_copy(sd.at[:, block(t, wide)], dbuf.at[t % depth], dsem.at[t % depth])

    def result(t):
        return pltpu.make_async_copy(ybuf.at[t % 2], y.at[:, block(t, wide)], ysem.at[t % 2])

    load = pltpu.make_async_copy(x, xv, xsem)
    load.start()
    for i in range(depth):
        for c in up(i):
            c.start()
    load.wait()
    split = pltpu.make_async_copy(xv.at[:, x.shape[1] - rest.shape[1] :], rest, xsem)
    split.start()

    def raise_(i, _):
        for c in up(i):
            c.wait()
        gu = jnp.dot(xv[...], wbuf[i % depth], preferred_element_type=F32)
        hbuf[:, block(i, tile)] = (jax.nn.silu(gu[:, :tile]) * gu[:, tile:]).astype(BF16)

        @pl.when(i + depth < ups)
        def _():
            for c in up(i + depth):
                c.start()

        @pl.when(i >= ups - depth)
        def _():
            down(i - (ups - depth)).start()

        return 0

    lax.fori_loop(0, ups, raise_, 0)

    def lower(t, _):
        down(t).wait()

        @pl.when(t >= 2)
        def _():
            result(t - 2).wait()

        ybuf[t % 2] = jnp.dot(hbuf[...], dbuf[t % depth], preferred_element_type=F32)
        result(t).start()

        @pl.when(t + depth < downs)
        def _():
            down(t + depth).start()

        return 0

    lax.fori_loop(0, downs, lower, 0)
    for t in (downs - 2, downs - 1):
        result(t).wait()
    split.wait()


def shared_call(x, sg, su, sd):
    tokens, rows = x.shape
    ff, width = sd.shape
    tile, wide, depth = 256, 1024, 4
    return pl.pallas_call(
        functools.partial(shared_kernel, tile, wide, depth),
        out_shape=[
            jax.ShapeDtypeStruct((tokens, width), F32),
            jax.ShapeDtypeStruct((tokens, rows - FIRST), BF16),
        ],
        in_specs=[ANY] * 4,
        out_specs=[ANY] * 2,
        scratch_shapes=[
            pltpu.VMEM((tokens, rows), BF16),
            pltpu.VMEM((depth, rows, 2 * tile), BF16),
            pltpu.VMEM((depth, ff, wide), BF16),
            pltpu.VMEM((tokens, ff), BF16),
            pltpu.VMEM((2, tokens, wide), F32),
            pltpu.SemaphoreType.DMA,
            pltpu.SemaphoreType.DMA((depth, 2)),
            pltpu.SemaphoreType.DMA((depth,)),
            pltpu.SemaphoreType.DMA((2,)),
        ],
        compiler_params=pltpu.CompilerParams(vmem_limit_bytes=63 * 2**20),
        cost_estimate=pl.CostEstimate(
            flops=6 * tokens * rows * ff, bytes_accessed=6 * rows * ff, transcendentals=0
        ),
        name="shared",
    )(x, sg, su, sd)


def down_kernel(tile, small, table, h, wd, shared, y, hv, wbuf, rows, mix, own, far32, outs, lands, sbuf, ybuf, hsem, wsem, ssem, ysem, send, recv):
    experts, _, width = wd.shape
    _, room = mix.shape[1:]
    pairs = experts // 2
    many = width // tile - 1
    few = tile // small
    me = lax.axis_index("ep")
    near, far = me + 1 - 2 * (me % 2), (me + 2) % 4

    barrier = pltpu.get_barrier_semaphore()
    for d in (near, far):
        pl.semaphore_signal(barrier, inc=1, device_id={"ep": d}, device_id_type=MESH)

    class Tile:
        def __init__(self, t, part=None):
            self.t = t if part is None else many + part
            self.n = tile if part is None else small
            start = t * tile if part is None else many * tile + part * small
            self.columns = pl.ds(pl.multiple_of(start, small), self.n)
            self.place = t if part is None else many
            self.inside = pl.ds(0 if part is None else part * small, self.n)

        def addend(self):
            s = self.t % 2
            return pltpu.make_async_copy(shared.at[:, self.columns], sbuf.at[s, :, : self.n], ssem.at[s])

        def result(self):
            s = self.t % 2
            return pltpu.make_async_copy(ybuf.at[s, :, : self.n], y.at[:, self.columns], ysem.at[s])

        def sending(self, kind):
            return pltpu.make_async_remote_copy(
                src_ref=outs.at[kind, self.t % 2, :, : self.n],
                dst_ref=lands.at[kind, self.place, :, self.inside],
                send_sem=send.at[kind, self.t],
                recv_sem=recv.at[kind, self.t],
                device_id={"ep": far if kind == 2 else near},
                device_id_type=MESH,
            )

        def combine(self, older):
            n, s = self.n, self.t % 2

            def free(old):
                old.sending(0).wait_send()
                old.sending(1).wait_send()

            older(free)
            outs[0, s, :, :n] = jnp.dot(mix[1], rows[1, :, :n], preferred_element_type=F32).astype(BF16)
            outs[1, s, :, :n] = jnp.dot(mix[3], rows[3, :, :n], preferred_element_type=F32).astype(BF16)
            far32[s, :, :n] = jnp.dot(mix[2], rows[2, :, :n], preferred_element_type=F32)
            own[self.t % 4, :, :n] = jnp.dot(mix[0], rows[0, :, :n], preferred_element_type=F32)
            self.sending(1).start()
            self.sending(0).start()

        def forward(self, older):
            n, s = self.n, self.t % 2
            self.sending(1).wait_recv()
            older(lambda old: old.sending(2).wait_send())
            outs[2, s, :, :n] = (far32[s, :, :n] + lands[1, self.place, :, self.inside].astype(F32)).astype(BF16)
            self.sending(2).start()

        def final(self, older, newer):
            n, s = self.n, self.t % 2
            self.sending(0).wait_recv()
            self.sending(2).wait_recv()
            self.addend().wait()
            older(lambda old: old.result().wait())
            local = own[self.t % 4, :, :n] + sbuf[s, :, :n]
            rest = (lands[k, self.place, :, self.inside].astype(F32) for k in (0, 2))
            ybuf[s, :, :n] = (local + next(rest) + next(rest)).astype(BF16)
            self.result().start()
            newer(lambda new: new.addend().start())

    def weights(t, p):
        q = (t.t * pairs + p) % 2
        return [
            pltpu.make_async_copy(
                wd.at[2 * p + m, :, t.columns], wbuf.at[2 * q + m, :, : t.n], wsem.at[2 * q + m]
            )
            for m in range(2)
        ]

    def start(copies):
        for c in copies:
            c.start()

    def load(e):
        return pltpu.make_async_copy(h.at[e], hv.at[e], hsem.at[e])

    def multiply(t, p):
        q = (t.t * pairs + p) % 2
        for c in weights(t, p):
            c.wait()
        for m in range(2):
            e = 2 * p + m
            o = jnp.dot(hv[e], wbuf[2 * q + m, :, : t.n], preferred_element_type=F32).astype(BF16)
            for k in range(4):
                rows[k, pl.ds(pl.multiple_of(e * SEG, 16), SEG), : t.n] = o[SEG * k : SEG * (k + 1)]

    for p in range(2):
        load(2 * p).start()
        load(2 * p + 1).start()
        start(weights(Tile(0), p))
    for e in range(4, experts):
        load(e).start()
    for t in range(2):
        Tile(t).addend().start()

    place, row = (lax.broadcasted_iota(jnp.int32, (experts, room), d) for d in (1, 0))
    spread = jnp.where((place >= SEG * row) & (place < SEG * (row + 1)), 1.0, 0.0).astype(BF16)
    place = lax.broadcasted_iota(jnp.int32, (1, room), 1)
    slot = place
    for e in range(1, experts):
        slot = jnp.where(place >= SEG * e, place - SEG * e, slot)
    slot = slot.astype(F32)
    for k in range(4):
        s, g = (
            lax.dot_general(table[k, n].astype(BF16), spread, (((0,), (0,)), ((), ())), preferred_element_type=F32)
            for n in range(2)
        )
        mix[k] = jnp.where(s == slot, g, 0.0).astype(BF16)
    pl.semaphore_wait(barrier, 2)

    def step(i, _):
        t, p = i // pairs, i % pairs
        this = Tile(t)

        def back(least, distance):
            def older(act):
                @pl.when(t >= least)
                def _():
                    act(Tile(t - distance))

            return older

        @pl.when(t == 0)
        def _():
            load(2 * p).wait()
            load(2 * p + 1).wait()

        multiply(this, p)

        @pl.when(i + 2 < many * pairs)
        def _():
            start(weights(Tile((i + 2) // pairs), (i + 2) % pairs))

        @pl.when(i + 2 >= many * pairs)
        def _():
            start(weights(Tile(0, 0), i + 2 - many * pairs))

        @pl.when((p == 0) & (t >= 1))
        def _():
            Tile(t - 1).forward(back(3, 3))

        @pl.when((p == 2) & (t >= 2))
        def _():
            Tile(t - 2).final(back(4, 4), lambda act: act(Tile(t)))

        @pl.when(p == pairs - 1)
        def _():
            this.combine(back(2, 2))

        return 0

    lax.fori_loop(0, many * pairs, step, 0)

    tiles = [Tile(t) for t in range(many)] + [Tile(0, m) for m in range(few)]

    def at(n):
        return lambda act: act(tiles[n])

    for n in range(many, many + few):

        def step2(p, _):
            multiply(tiles[n], p)

            @pl.when(p + 2 < pairs)
            def _():
                start(weights(tiles[n], p + 2))

            if n + 1 < many + few:

                @pl.when(p + 2 >= pairs)
                def _():
                    start(weights(tiles[n + 1], p + 2 - pairs))

            @pl.when(p == 0)
            def _():
                tiles[n - 1].forward(at(n - 3))

            @pl.when(p == 2)
            def _():
                tiles[n - 2].final(at(n - 4), at(n))

            return 0

        lax.fori_loop(0, pairs, step2, 0)
        tiles[n].combine(at(n - 2))
    last = many + few - 1
    tiles[last].forward(at(last - 2))
    tiles[last - 1].final(at(last - 3), lambda act: None)
    tiles[last].final(at(last - 2), lambda act: None)
    for t in tiles[-2:]:
        t.result().wait()
        for kind in range(3):
            t.sending(kind).wait_send()


def down_call(table, h, wd, shared):
    experts, ff, width = wd.shape
    tile, small = 1024, 512
    tiles = width // tile
    count = tiles - 1 + tile // small
    tokens = table.shape[3]
    room = SEG * experts
    return pl.pallas_call(
        functools.partial(down_kernel, tile, small),
        out_shape=jax.ShapeDtypeStruct((tokens, width), BF16),
        in_specs=[VMEM, ANY, ANY, ANY],
        out_specs=ANY,
        scratch_shapes=[
            pltpu.VMEM((experts, 4 * SEG, ff), BF16),
            pltpu.VMEM((4, ff, tile), BF16),
            pltpu.VMEM((4, room, tile), BF16),
            pltpu.VMEM((4, tokens, room), BF16),
            pltpu.VMEM((4, tokens, tile), F32),
            pltpu.VMEM((2, tokens, tile), F32),
            pltpu.VMEM((3, 2, tokens, tile), BF16),
            pltpu.VMEM((3, tiles, tokens, tile), BF16),
            pltpu.VMEM((2, tokens, tile), F32),
            pltpu.VMEM((2, tokens, tile), BF16),
            pltpu.SemaphoreType.DMA((experts,)),
            pltpu.SemaphoreType.DMA((4,)),
            pltpu.SemaphoreType.DMA((2,)),
            pltpu.SemaphoreType.DMA((2,)),
            pltpu.SemaphoreType.DMA((3, count)),
            pltpu.SemaphoreType.DMA((3, count)),
        ],
        compiler_params=pltpu.CompilerParams(vmem_limit_bytes=63 * 2**20, collective_id=0, has_side_effects=True),
        cost_estimate=pl.CostEstimate(
            flops=2 * experts * 4 * SEG * width * ff, bytes_accessed=experts * width * ff * 2, transcendentals=0
        ),
        name="down",
    )(table, h, wd, shared)


def solution(mesh):
    members = mesh.shape["ep"]

    def move(v, hop):
        return lax.ppermute(v, "ep", [(i, i ^ hop) for i in range(members)])

    def body(x, expert, slot, gate, wg, wu, wd, sg, su, sd):
        x, expert, slot, gate = (v[0, 0] for v in (x, expert, slot, gate))
        local = wg.shape[0]
        me = lax.axis_index("ep")

        hit = (expert.T[None] == jnp.arange(local * members)[:, None, None]) & (slot.T < SEG)[None]
        slots = jnp.max(jnp.where(hit, slot.T[None], -1), axis=1)
        gates = jnp.sum(jnp.where(hit, gate.T.astype(BF16).astype(F32)[None], 0.0), axis=1)
        table = jnp.stack([slots.astype(F32), gates])
        parts = []
        for hop in range(members):
            part = lax.dynamic_slice_in_dim(table, (me ^ hop) * local, local, axis=1)
            parts.append(move(part, hop) if hop else part)

        far = [move(x[:, :FIRST], 2)]
        near = move(x, 1)

        shared, rest_x = shared_call(x, sg, su, sd)
        far.append(move(rest_x, 2))

        shared, far[0] = lax.optimization_barrier((shared, far[0]))
        table = jnp.stack(parts)
        npad = (jnp.max(table[:, 0], axis=2).astype(jnp.int32) + 16) // 16 * 16
        sums = up_call(0, FIRST, npad, table, (x, near, far[0], move(far[0], 1)), wg, wu)
        sums, far[1] = lax.optimization_barrier((sums, far[1]))
        rest = x.shape[1] - FIRST
        h = up_call(FIRST, rest, npad, table, (x, near, far[1], move(far[1], 1)), wg, wu, sums)
        return down_call(table, h, wd, shared)[None, None]

    tok, exp, whole = P("dp", "ep", None, None), P("ep", None, None), P(None, None)

    return jax.shard_map(
        body,
        mesh=mesh,
        in_specs=(tok, tok, tok, tok, exp, exp, exp, whole, whole, whole),
        out_specs=tok,
        check_vma=False,
    )
```

time: 398 us -> 366 us (0.920)
  the two profiles are of different devices: /device:TPU:6 before, /device:TPU:0 now
where the time goes in v2:
time: 366 us; the launch traced here: 364 us
  Pallas kernels  343 us (94%)
  waiting for transfers between devices  7.09 us (2%)
  local copies, waits for them, and re-layouts  6.56 us (2%)
  starting transfers between devices  5.61 us (2%)
    pallas_call x1, Pallas kernels, down_call(): pl.pallas_call(functools.partial(down_kernel, tile, small), out_shape=jax...  130 us
    pallas_call x1, Pallas kernels, up_call(): pl.pallas_call(functools.partial(up_kernel, first, tile, depth), out_shap...  117 us
    pallas_call x1, Pallas kernels, up_call(): pl.pallas_call(functools.partial(begin_kernel, tile, depth), out_shape=ja...  59.7 us
    pallas_call x1, Pallas kernels, shared_call(): pl.pallas_call(functools.partial(shared_kernel, tile, wide, depth), out_s...  36 us
  transfers between devices with their start and end apart: 8, of which 3 were waited for; matrix products, arithmetic and copies ran while one was open for 1% of the time, Pallas kernels for 26%

profile of v2, /device:TPU:0, one launch (start us, length us, event | category | flops | bytes accessed | tf_op | source)
XLA Modules:
  0.0 364.2 jit_solution(16181325337845147161)
XLA Ops:
  0.0 0.8 collective-permute-start.3
  0.8 2.4 slice.9
  3.3 2.5 collective-permute-start.4
  5.7 0.7 convert_bitcast_fusion.1
  6.4 36.0 %shared.1 = (f32[256,7168]{1,0:T(8,128)}, bf16[256,4864]{1,0:T(8,128)(2,1)}) custom-call(bf16[256,7168]{1,0:T(8,128)(2,1)} %bitcast.24, bf16[7168,2048]{1,0:T(8,128)(2,1)} %sg.1, bf16[7168,2048]{1,0:T(8,128)(2,1)} %su.1, bf16[2048,7168]{1,0:T(8,128)(2,1)} %sd.1), custom_call_target="tpu_custom_call" | custom-call | flops 22548578304 | bytes 88080384 | tf_op jit(solution)/shard_map/shared/pallas_call | solution.py:281
  42.5 0.0 collective-permute-done.4.x2
  42.5 0.2 collective-permute-start.5
  42.7 0.1 select_reduce_fusion
  42.9 0.1 select_reduce_fusion.1
  43.0 0.3 collective-permute-start
  43.4 0.0 collective-permute-start.1
  43.4 1.5 collective-permute-start.2
  44.9 0.8 collective-permute-done
  45.7 0.1 collective-permute-start.6
  45.8 1.3 collective-permute-done.1
  47.1 0.0 collective-permute-done.2
  47.1 0.1 slice_reduce_fusion
  47.2 0.6 fusion.7.npad
  47.8 59.7 %up_first.1.refs_0_ = f32[8,8,320,512]{3,2,1,0:T(8,128)} custom-call(s32[4,8]{1,0:T(4,128)} %fusion.7.npad, f32[4,2,8,256]{3,2,1,0:T(8,128)} %copy-done, bf16[256,7168]{1,0:T(8,128)(2,1)} %bitcast.25, bf16[256,7168]{1,0:T(8,128)(2,1)} %collective-permute-done.3.x1, bf16[256,2304]{1,0:T(8,128)(2,1)} %collective-permute-done.4.x2, ...), custom_call_target="tpu_custom_call" | custom-call | flops 24159191040 | bytes 150994944 | tf_op jit(solution)/shard_map/up_first/pallas_call | solution.py:183
  107.5 0.0 collective-permute-start.7
  107.5 5.0 %collective-permute-done.7.x3 = bf16[256,4864]{1,0:T(8,128)(2,1)} collective-permute-done((bf16[256,4864]{1,0:T(8,128)(2,1)}, bf16[256,4864]{1,0:T(8,128)(2,1)}, u32[]{:S(2)}, u32[]{:S(2)}) %collective-permute-start.7) | collective-permute-done | bytes 2490400 | tf_op jit(solution)/shard_map/ppermute | solution.py:559
  112.6 117.5 %up_rest.1.h = bf16[8,320,2048]{2,1,0:T(8,128)(2,1)} custom-call(s32[4,8]{1,0:T(4,128)} %fusion.7.npad, f32[4,2,8,256]{3,2,1,0:T(8,128)} %copy-done, bf16[256,7168]{1,0:T(8,128)(2,1)} %bitcast.26, bf16[256,7168]{1,0:T(8,128)(2,1)} %collective-permute-done.3.x1, bf16[256,4864]{1,0:T(8,128)(2,1)} %collective-permute-done.6.x2, ...), custom_call_target="tpu_custom_call" | custom-call | flops 51002736640 | bytes 318767104 | tf_op jit(solution)/shard_map/up_rest/pallas_call | solution.py:192
  230.0 130.0 %down.1 = bf16[256,7168]{1,0:T(8,128)(2,1)} custom-call(f32[4,2,8,256]{3,2,1,0:T(8,128)} %copy-done, bf16[8,320,2048]{2,1,0:T(8,128)(2,1)} %up_rest.1.h, bf16[8,2048,7168]{2,1,0:T(8,128)(2,1)} %wd.1, f32[256,7168]{1,0:T(8,128)} %get-tuple-element.16.shared), custom_call_target="tpu_custom_call" | custom-call | flops 75161927680 | bytes 234881024 | tf_op jit(solution)/shard_map/down/pallas_call | solution.py:524
  360.1 4.1 %copy.12 = bf16[1,1,256,7168]{3,2,1,0:T(8,128)(2,1)} copy(bf16[1,1,256,7168]{3,2,1,0:T(8,128)(2,1)} %bitcast.27) | data formatting | bytes 7340032
  (13 shorter events, 0.1 us)
Async XLA Ops:
  0.0 47.8 %collective-permute-start.3 = (bf16[256,7168]{1,0:T(8,128)(2,1)}, bf16[256,7168]{1,0:T(8,128)(2,1)}, u32[]{:S(2)}, u32[]{:S(2)}) collective-permute-start(bf16[256,7168]{1,0:T(8,128)(2,1)} %bitcast.22), channel_id=1, source_target_pairs={{0,1},{1,0},{2,3},{3,2},{4,5},{5,4},{6,7},{7,6}} | collective-permute-start | bytes 11010056 | tf_op jit(solution)/shard_map/ppermute | solution.py:559
  3.3 39.2 %collective-permute-start.4 = (bf16[256,2304]{1,0:T(8,128)(2,1)}, bf16[256,2304]{1,0:T(8,128)(2,1)}, u32[]{:S(2)}, u32[]{:S(2)}) collective-permute-start(bf16[256,2304]{1,0:T(8,128)(2,1)} %slice.9), channel_id=1, source_target_pairs={{0,2},{1,3},{2,0},{3,1},{4,6},{5,7},{6,4},{7,5}} | collective-permute-start | bytes 3538952 | tf_op jit(solution)/shard_map/ppermute | solution.py:559
  6.4 36.3 %copy-start.1 = (s32[1,1,256,8]{2,3,1,0:T(8,128)S(1)}, s32[1,1,256,8]{2,3,1,0:T(8,128)}, u32[]{:S(2)}) copy-start(s32[1,1,256,8]{2,3,1,0:T(8,128)} %param.12) | copy-start | bytes 24580
  6.4 36.3 %copy-start.2 = (s32[1,1,256,8]{2,3,1,0:T(8,128)S(1)}, s32[1,1,256,8]{2,3,1,0:T(8,128)}, u32[]{:S(2)}) copy-start(s32[1,1,256,8]{2,3,1,0:T(8,128)} %param.11) | copy-start | bytes 24580
  42.5 5.3 %collective-permute-start.5 = (bf16[256,2304]{1,0:T(8,128)(2,1)}, bf16[256,2304]{1,0:T(8,128)(2,1)}, u32[]{:S(2)}, u32[]{:S(2)}) collective-permute-start(bf16[256,2304]{1,0:T(8,128)(2,1)} %collective-permute-done.4.x2), channel_id=1, source_target_pairs={{0,1},{1,0},{2,3},{3,2},{4,5},{5,4},{6,7},{7,6}} | collective-permute-start | bytes 3538952 | tf_op jit(solution)/shard_map/ppermute | solution.py:559
  43.0 2.6 collective-permute-start
  43.4 3.7 %collective-permute-start.1 = (f32[2,8,256]{2,1,0:T(8,128)S(1)}, f32[2,8,256]{2,1,0:T(8,128)S(1)}, u32[]{:S(2)}, u32[]{:S(2)}) collective-permute-start(f32[2,8,256]{2,1,0:T(8,128)S(1)} %get-tuple-element.19), channel_id=1, source_target_pairs={{0,2},{1,3},{2,0},{3,1},{4,6},{5,7},{6,4},{7,5}} | collective-permute-start | bytes 49160 | tf_op jit(solution)/shard_map/ppermute | solution.py:559
  43.4 3.7 %collective-permute-start.2 = (f32[2,8,256]{2,1,0:T(8,128)S(1)}, f32[2,8,256]{2,1,0:T(8,128)S(1)}, u32[]{:S(2)}, u32[]{:S(2)}) collective-permute-start(f32[2,8,256]{2,1,0:T(8,128)S(1)} %get-tuple-element.20), channel_id=1, source_target_pairs={{0,3},{1,2},{2,1},{3,0},{4,7},{5,6},{6,5},{7,4}} | collective-permute-start | bytes 49160 | tf_op jit(solution)/shard_map/ppermute | solution.py:559
  45.7 61.8 %collective-permute-start.6 = (bf16[256,4864]{1,0:T(8,128)(2,1)}, bf16[256,4864]{1,0:T(8,128)(2,1)}, u32[]{:S(2)}, u32[]{:S(2)}) collective-permute-start(bf16[256,4864]{1,0:T(8,128)(2,1)} %get-tuple-element.13), channel_id=1, source_target_pairs={{0,2},{1,3},{2,0},{3,1},{4,6},{5,7},{6,4},{7,5}} | collective-permute-start | bytes 7471112 | tf_op jit(solution)/shard_map/ppermute | solution.py:559
  47.1 0.7 copy-start
  107.5 5.1 %collective-permute-start.7 = (bf16[256,4864]{1,0:T(8,128)(2,1)}, bf16[256,4864]{1,0:T(8,128)(2,1)}, u32[]{:S(2)}, u32[]{:S(2)}) collective-permute-start(bf16[256,4864]{1,0:T(8,128)(2,1)} %collective-permute-done.6.x2), channel_id=1, source_target_pairs={{0,1},{1,0},{2,3},{3,2},{4,5},{5,4},{6,7},{7,6}} | collective-permute-start | bytes 7471112 | tf_op jit(solution)/shard_map/ppermute | solution.py:559

commit v3 on v2

--- a/solution.py
+++ b/solution.py
@@ -8,7 +8,8 @@
 from jax.sharding import PartitionSpec as P
 
 
-FIRST = 2304
+FIRST = 3328
+EARLY = 4
 UNIT = 256
 HALF = 160
 SEG = 80
@@ -27,179 +28,276 @@
     return offs, total
 
 
-def up_kernel(first, tile, depth, npad, table, x0, x1, x2, x3, wg, wu, *refs):
-    (sums, h, xv, z, wbuf, abuf, hbuf, hout, xsem, wsem, asem, hsem), begins = refs, first == 0
-    experts, ff, rows = wg.shape[0], wg.shape[2], z.shape[1]
-    per = ff // tile
+def place(offs, k):
+    return pl.ds(pl.multiple_of(offs[k], 16), SEG)
+
+
+def dispatch(npad, table, e, xv, z):
+    offs, _ = offsets(npad, e)
+    line = lax.broadcasted_iota(jnp.int32, (SEG, table.shape[3]), 0).astype(F32)
+    for k in range(4):
+        pick = jnp.where(line == table[k, 0, pl.ds(e, 1), :], 1.0, 0.0).astype(BF16)
+        z[place(offs, k), :] = jnp.dot(pick, xv[k], preferred_element_type=F32).astype(BF16)
+
+
+def for_rows(total, work):
+    for low, high in ((n, n + SEG) for n in range(0, 4 * SEG, SEG)):
+
+        @pl.when((total > low) & (total <= high))
+        def _():
+            work(high)
+
+
+def arrange(npad, experts, order):
+    half = experts // 2
+    totals = [offsets(npad, e)[1] for e in range(experts)]
+    for e in range(experts):
+        rank = jnp.int32(0)
+        for o in range(experts):
+            if o != e:
+                ahead = totals[o] >= totals[e] if o < e else totals[o] > totals[e]
+                rank = rank + ahead.astype(jnp.int32)
+        order[jnp.where(rank < half, 2 * (half - 1 - rank), 2 * (rank - half) + 1)] = e
+
+
+def sums_copies(npad, e, near, away, sem, act, out):
+    _, total = offsets(npad, e)
+    for b in range(4):
+        band = pl.ds(b * SEG, SEG)
+
+        @pl.when(total > b * SEG)
+        def _():
+            pair = near.at[:, band], away.at[:, band]
+            act(pltpu.make_async_copy(*(pair if out else pair[::-1]), sem.at[b]))
+
+
+def start(copy):
+    copy.start()
+
+
+def wait(copy):
+    copy.wait()
+
+
+def first_kernel(tile, depth, npad, table, x0, x1, x2, x3, wg, wu, sums, xv, z, wbuf, abuf, order, xsem, wsem, asem):
+    experts, rows = sums.shape[0], z.shape[1]
+    per = wg.shape[2] // tile
     steps = experts * per
     units = tile // UNIT
-    ring = abuf.shape[0]
 
     def weights(i):
-        e, cols, s = i // per, pl.ds(pl.multiple_of((i % per) * tile, tile), tile), i % depth
+        e, cols, s = order[i // per], pl.ds(pl.multiple_of((i % per) * tile, tile), tile), i % depth
         return [
             pltpu.make_async_copy(
-                w.at[e, pl.ds(first, rows), cols], wbuf.at[s, :, pl.ds(n * tile, tile)], wsem.at[s, n]
+                w.at[e, pl.ds(0, rows), cols], wbuf.at[s, n], wsem.at[s, n]
             )
             for n, w in enumerate((wg, wu))
         ]
 
-    def partial(i, act):
-        e, j, s = i // per, i % per, i % ring
-        _, total = offsets(npad, e)
-        for b in range(4):
-            band = pl.ds(b * SEG, SEG)
-            near, away = abuf.at[s, :, band], sums.at[e, pl.ds(j * units, units), band]
-
-            @pl.when(total > b * SEG)
-            def _():
-                act(pltpu.make_async_copy(*((near, away) if begins else (away, near)), asem.at[s, b]))
-
-    def result(e):
-        return pltpu.make_async_copy(hout.at[e % 2], h.at[e], hsem.at[e % 2])
-
-    def ask(i):
-        for c in weights(i):
-            c.start()
-        if not begins:
-            partial(i, lambda c: c.start())
+    def keep(i, act):
+        e, s = order[i // per], i % 2
+        sums_copies(npad, e, abuf.at[s], sums.at[i // per, pl.ds((i % per) * units, units)], asem.at[s], act, True)
 
     blocks = []
     for k, x in enumerate((x0, x1, x2, x3)):
-        part = x if x.shape[1] == rows else x.at[:, pl.ds(first, rows)]
+        part = x if x.shape[1] == rows else x.at[:, pl.ds(0, rows)]
         blocks.append(pltpu.make_async_copy(part, xv.at[k], xsem.at[k]))
     for c in blocks:
         c.start()
+    arrange(npad, wg.shape[0], order)
     for i in range(depth):
-        ask(i)
+        for c in weights(i):
+            c.start()
     for c in blocks:
         c.wait()
 
-    def dispatch(e):
-        offs, _ = offsets(npad, e)
-        line = lax.broadcasted_iota(jnp.int32, (SEG, xv.shape[1]), 0).astype(F32)
-        for k in range(4):
-            pick = jnp.where(line == table[k, 0, pl.ds(e, 1), :], 1.0, 0.0).astype(BF16)
-            at = pl.ds(pl.multiple_of(offs[k], 16), SEG)
-            z[at, :] = jnp.dot(pick, xv[k], preferred_element_type=F32).astype(BF16)
-
     def step(i, _):
-        e, j, s, a = i // per, i % per, i % depth, i % ring
-        offs, total = offsets(npad, e)
-
-        @pl.when(j == 0)
-        def _():
-            dispatch(e)
+        e, s = order[i // per], i % depth
+        _, total = offsets(npad, e)
+
+        @pl.when(i % per == 0)
+        def _():
+            dispatch(npad, table, e, xv, z)
 
         for c in weights(i):
             c.wait()
-        if begins:
-
-            @pl.when(i >= ring)
+
+        @pl.when(i >= 2)
+        def _():
+            keep(i - 2, wait)
+
+        def work(n):
+            for m in range(2):
+                half = jnp.dot(z[:n, :], wbuf[s, m], preferred_element_type=F32)
+                for v in range(units):
+                    abuf[i % 2, v, :n, m * UNIT : (m + 1) * UNIT] = half[:, v * UNIT : (v + 1) * UNIT]
+
+        for_rows(total, work)
+
+        @pl.when(i + depth < steps)
+        def _():
+            for c in weights(i + depth):
+                c.start()
+
+        keep(i, start)
+        return 0
+
+    lax.fori_loop(0, steps, step, 0)
+    for i in (steps - 2, steps - 1):
+        keep(jnp.int32(i), wait)
+
+
+def rest_kernel(depth, npad, table, x0, x1, f0, d0, f1, d1, wg, wu, sums, h, xv, z, wbuf, abuf, hbuf, hout, order, xsem, wsem, asem, hsem):
+    experts, rows, ff = wg.shape
+    part = sums.shape[0]
+    first = f0.shape[1]
+    per = ff // UNIT
+    begun, steps = part * per, experts * per
+
+    def weights(i, low):
+        e, cols, s = order[i // per], pl.ds(pl.multiple_of((i % per) * UNIT, UNIT), UNIT), i % depth
+        band = pl.ds(low, rows - low)
+        return [
+            pltpu.make_async_copy(w.at[e, band, cols], wbuf.at[s, n, band], wsem.at[s, n])
+            for n, w in enumerate((wg, wu))
+        ]
+
+    def resume(i, act):
+        e, s = order[i // per], i % depth
+        sums_copies(npad, e, abuf.at[pl.ds(s, 1)], sums.at[i // per, pl.ds(i % per, 1)], asem.at[s], act, False)
+
+    def ask(i, low):
+        for c in weights(i, low):
+            c.start()
+        if low:
+            resume(i, start)
+
+    def result(n):
+        return pltpu.make_async_copy(hout.at[n % 2], h.at[order[n]], hsem.at[n % 2])
+
+    blocks = [pltpu.make_async_copy(x, xv.at[k], xsem.at[k]) for k, x in enumerate((x0, x1))]
+    for n, (a, b) in enumerate(((f0, f1), (d0, d1))):
+        blocks.append(pltpu.make_async_copy(a, xv.at[2 + n, :, pl.ds(0, first)], xsem.at[2 + 2 * n]))
+        blocks.append(pltpu.make_async_copy(b, xv.at[2 + n, :, pl.ds(first, rows - first)], xsem.at[3 + 2 * n]))
+    for c in blocks:
+        c.start()
+    arrange(npad, experts, order)
+    for i in range(depth):
+        ask(i, first)
+    for c in blocks:
+        c.wait()
+
+    def step(low, i):
+        n, j, s = i // per, i % per, i % depth
+        e = order[n]
+        offs, total = offsets(npad, e)
+
+        @pl.when(j == 0)
+        def _():
+            dispatch(npad, table, e, xv.at[:, :, low:], z.at[:, low:])
+
+        for c in weights(i, low):
+            c.wait()
+        if low:
+            resume(i, wait)
+
+        def work(n):
+            g, u = (jnp.dot(z[:n, low:], wbuf[s, m, low:], preferred_element_type=F32) for m in range(2))
+            if low:
+                g, u = g + abuf[s, :n, :UNIT], u + abuf[s, :n, UNIT:]
+            hbuf[:n, pl.ds(pl.multiple_of(j * UNIT, UNIT), UNIT)] = (jax.nn.silu(g) * u).astype(BF16)
+
+        for_rows(total, work)
+
+        if low:
+
+            @pl.when(i + depth < begun)
             def _():
-                partial(i - ring, lambda c: c.wait())
+                ask(i + depth, low)
+
+            @pl.when(i + depth >= begun)
+            def _():
+                ask(i + depth, 0)
         else:
-            partial(i, lambda c: c.wait())
-
-        def work(n):
-            gu = jnp.dot(z[:n, :], wbuf[s], preferred_element_type=F32)
-            for v in range(units):
-                g, u = (gu[:, m * tile + v * UNIT :][:, :UNIT] for m in range(2))
-                if begins:
-                    abuf[a, v, :n, :UNIT] = g
-                    abuf[a, v, :n, UNIT:] = u
-                else:
-                    g, u = g + abuf[a, v, :n, :UNIT], u + abuf[a, v, :n, UNIT:]
-                    cols = pl.ds(pl.multiple_of(j * tile + v * UNIT, UNIT), UNIT)
-                    hbuf[:n, cols] = (jax.nn.silu(g) * u).astype(BF16)
-
-        @pl.when((total > 0) & (total <= HALF))
-        def _():
-            work(HALF)
-
-        @pl.when(total > HALF)
-        def _():
-            work(2 * HALF)
-
-        @pl.when(i + depth < steps)
-        def _():
-            ask(i + depth)
-
-        if begins:
-            partial(i, lambda c: c.start())
-            return 0
+
+            @pl.when(i + depth < steps)
+            def _():
+                ask(i + depth, 0)
 
         @pl.when(j == per - 1)
         def _():
-            @pl.when(e >= 2)
+            @pl.when(n >= 2)
             def _():
-                result(e).wait()
+                result(n - 2).wait()
 
             line = lax.broadcasted_iota(jnp.int32, (SEG, ff), 0)
             for k in range(4):
-                part = hbuf[pl.ds(pl.multiple_of(offs[k], 16), SEG), :]
-                hout[e % 2, SEG * k : SEG * (k + 1), :] = jnp.where(line < npad[k, e], part, jnp.zeros_like(part))
-            result(e).start()
+                band = hbuf[place(offs, k), :]
+                hout[n % 2, SEG * k : SEG * (k + 1), :] = jnp.where(line < npad[k, e], band, jnp.zeros_like(band))
+            result(n).start()
 
         return 0
 
-    lax.fori_loop(0, steps, step, 0)
-    if begins:
-        for i in range(steps - ring, steps):
-            partial(jnp.int32(i), lambda c: c.wait())
-    else:
-        for e in (experts - 2, experts - 1):
-            result(e).wait()
-
-
-def begin_kernel(tile, depth, npad, table, x0, x1, x2, x3, wg, wu, sums, xv, z, wbuf, abuf, xsem, wsem, asem):
-    refs = (sums, None, xv, z, wbuf, abuf, None, None, xsem, wsem, asem, None)
-    up_kernel(0, tile, depth, npad, table, x0, x1, x2, x3, wg, wu, *refs)
-
-
-def up_call(first, rows, npad, table, xs, wg, wu, sums=None):
-    experts, _, ff = wg.shape
-    tile, depth = (512, 4) if first == 0 else (512, 3)
-    ring, units = (2 if first == 0 else depth), tile // UNIT
-    tokens = xs[0].shape[0]
-    scratch = [
-        pltpu.VMEM((4, tokens, rows), BF16),
-        pltpu.VMEM((2 * HALF, rows), BF16),
-        pltpu.VMEM((depth, rows, 2 * tile), BF16),
-        pltpu.VMEM((ring, units, 2 * HALF, 2 * UNIT), F32),
-    ]
-    semaphores = [
-        pltpu.SemaphoreType.DMA((4,)),
-        pltpu.SemaphoreType.DMA((depth, 2)),
-        pltpu.SemaphoreType.DMA((ring, 4)),
-    ]
-    common = dict(
+    lax.fori_loop(0, begun, lambda i, _: step(first, i), 0)
+    lax.fori_loop(begun, steps, lambda i, _: step(0, i), 0)
+    for n in (experts - 2, experts - 1):
+        result(n).wait()
+
+
+def expert_params(experts, rows, ff):
+    return dict(
         compiler_params=pltpu.CompilerParams(vmem_limit_bytes=63 * 2**20),
         cost_estimate=pl.CostEstimate(
-            flops=2 * experts * HALF * rows * ff * 2, bytes_accessed=experts * rows * ff * 4, transcendentals=0
+            flops=4 * experts * HALF * rows * ff, bytes_accessed=experts * rows * ff * 4, transcendentals=0
         ),
     )
-    if first == 0:
-        return pl.pallas_call(
-            functools.partial(begin_kernel, tile, depth),
-            out_shape=jax.ShapeDtypeStruct((experts, ff // UNIT, 2 * HALF, 2 * UNIT), F32),
-            in_specs=[SMEM, VMEM] + [ANY] * 6,
-            out_specs=ANY,
-            scratch_shapes=scratch + semaphores,
-            name="up_first",
-            **common,
-        )(npad, table, *xs, wg, wu)
+
+
+def first_call(experts, npad, table, xs, wg, wu):
+    ff, (tokens, rows) = wg.shape[2], xs[2].shape
+    tile, depth = 512, 3
     return pl.pallas_call(
-        functools.partial(up_kernel, first, tile, depth),
+        functools.partial(first_kernel, tile, depth),
+        out_shape=jax.ShapeDtypeStruct((experts, ff // UNIT, 2 * HALF, 2 * UNIT), F32),
+        in_specs=[SMEM, VMEM] + [ANY] * 6,
+        out_specs=ANY,
+        scratch_shapes=[
+            pltpu.VMEM((4, tokens, rows), BF16),
+            pltpu.VMEM((2 * HALF, rows), BF16),
+            pltpu.VMEM((depth, 2, rows, tile), BF16),
+            pltpu.VMEM((2, tile // UNIT, 2 * HALF, 2 * UNIT), F32),
+            pltpu.SMEM((wg.shape[0],), jnp.int32),
+            pltpu.SemaphoreType.DMA((4,)),
+            pltpu.SemaphoreType.DMA((depth, 2)),
+            pltpu.SemaphoreType.DMA((2, 4)),
+        ],
+        name="up_first",
+        **expert_params(experts, rows, ff),
+    )(npad, table, *xs, wg, wu)
+
+
+def rest_call(npad, table, xs, wg, wu, sums):
+    (experts, rows, ff), tokens, depth = wg.shape, xs[0].shape[0], 4
+    return pl.pallas_call(
+        functools.partial(rest_kernel, depth),
         out_shape=jax.ShapeDtypeStruct((experts, 2 * HALF, ff), BF16),
-        in_specs=[SMEM, VMEM] + [ANY] * 7,
+        in_specs=[SMEM, VMEM] + [ANY] * 9,
         out_specs=ANY,
-        scratch_shapes=scratch
-        + [pltpu.VMEM((2 * HALF, ff), BF16), pltpu.VMEM((2, 2 * HALF, ff), BF16)]
-        + semaphores
-        + [pltpu.SemaphoreType.DMA((2,))],
+        scratch_shapes=[
+            pltpu.VMEM((4, tokens, rows), BF16),
+            pltpu.VMEM((2 * HALF, rows), BF16),
+            pltpu.VMEM((depth, 2, rows, UNIT), BF16),
+            pltpu.VMEM((depth, 2 * HALF, 2 * UNIT), F32),
+            pltpu.VMEM((2 * HALF, ff), BF16),
+            pltpu.VMEM((2, 2 * HALF, ff), BF16),
+            pltpu.SMEM((experts,), jnp.int32),
+            pltpu.SemaphoreType.DMA((6,)),
+            pltpu.SemaphoreType.DMA((depth, 2)),
+            pltpu.SemaphoreType.DMA((depth, 4)),
+            pltpu.SemaphoreType.DMA((2,)),
+        ],
         name="up_rest",
-        **common,
+        **expert_params(experts, rows, ff),
     )(npad, table, *xs, wg, wu, sums)
 
 
@@ -581,10 +679,11 @@
         shared, far[0] = lax.optimization_barrier((shared, far[0]))
         table = jnp.stack(parts)
         npad = (jnp.max(table[:, 0], axis=2).astype(jnp.int32) + 16) // 16 * 16
-        sums = up_call(0, FIRST, npad, table, (x, near, far[0], move(far[0], 1)), wg, wu)
+        diag = [move(far[0], 1)]
+        sums = first_call(EARLY, npad, table, (x, near, far[0], diag[0]), wg, wu)
         sums, far[1] = lax.optimization_barrier((sums, far[1]))
-        rest = x.shape[1] - FIRST
-        h = up_call(FIRST, rest, npad, table, (x, near, far[1], move(far[1], 1)), wg, wu, sums)
+        diag.append(move(far[1], 1))
+        h = rest_call(npad, table, (x, near, far[0], diag[0], far[1], diag[1]), wg, wu, sums)
         return down_call(table, h, wd, shared)[None, None]
 
     tok, exp, whole = P("dp", "ep", None, None), P("ep", None, None), P(None, None)

time: 366 us -> 364 us (level)
  Pallas kernels: 343 us -> 335 us
    pallas_call x2, Pallas kernels: 177 us -> 170 us  [the longest x1 130 us: rest_call(): pl.pallas_call(functools.partial(rest_kernel, depth), out_shape=jax.Shape...]
  transfers between devices with their start and end apart: 8 -> 8, of which waited for: 3 -> 5; matrix products, arithmetic and copies ran while one was open for 1% -> 1% of each run, Pallas kernels for 26% -> 21%
where the time goes in v3:
time: 364 us; the launch traced here: 360 us
  Pallas kernels  335 us (92%)
  waiting for transfers between devices  10.6 us (3%)
  starting transfers between devices  7.33 us (2%)
  local copies, waits for them, and re-layouts  6.94 us (2%)
    pallas_call x1, Pallas kernels, rest_call(): pl.pallas_call(functools.partial(rest_kernel, depth), out_shape=jax.Shape...  130 us
    pallas_call x1, Pallas kernels, down_call(): pl.pallas_call(functools.partial(down_kernel, tile, small), out_shape=jax...  128 us
    pallas_call x1, Pallas kernels, first_call(): pl.pallas_call(functools.partial(first_kernel, tile, depth), out_shape=ja...  40 us
    pallas_call x1, Pallas kernels, shared_call(): pl.pallas_call(functools.partial(shared_kernel, tile, wide, depth), out_s...  36 us
    ppermute x8, waiting for transfers between devices, move(): return lax.ppermute(v, 'ep', [(i, i ^ hop) for i in range(members)])  10.6 us
    ppermute x8, starting transfers between devices, move(): return lax.ppermute(v, 'ep', [(i, i ^ hop) for i in range(members)])  7.33 us
  transfers between devices with their start and end apart: 8, of which 5 were waited for; matrix products, arithmetic and copies ran while one was open for 1% of the time, Pallas kernels for 21%

profile of v3, /device:TPU:0, one launch (start us, length us, event | category | flops | bytes accessed | tf_op | source)
XLA Modules:
  0.0 360.4 jit_solution(17018045190174040716)
XLA Ops:
  0.0 0.8 collective-permute-start.3
  0.8 2.8 slice.9
  3.7 2.5 collective-permute-start.4
  6.1 36.0 %shared.1 = (f32[256,7168]{1,0:T(8,128)}, bf16[256,3840]{1,0:T(8,128)(2,1)}) custom-call(bf16[256,7168]{1,0:T(8,128)(2,1)} %bitcast.24, bf16[7168,2048]{1,0:T(8,128)(2,1)} %sg.1, bf16[7168,2048]{1,0:T(8,128)(2,1)} %su.1, bf16[2048,7168]{1,0:T(8,128)(2,1)} %sd.1), custom_call_target="tpu_custom_call" | custom-call | flops 22548578304 | bytes 88080384 | tf_op jit(solution)/shard_map/shared/pallas_call | solution.py:379
  42.1 2.2 collective-permute-done.4.x2.f0
  44.3 0.0 collective-permute-start.5
  44.4 0.1 select_reduce_fusion
  44.5 0.1 select_reduce_fusion.1
  44.7 0.5 collective-permute-start
  45.2 1.7 collective-permute-start.1
  46.9 0.0 collective-permute-start.2
  46.9 1.3 collective-permute-done
  48.3 1.7 collective-permute-start.6
  50.0 0.0 collective-permute-done.1
  50.0 0.2 collective-permute-done.2
  50.2 0.1 slice_reduce_fusion
  50.3 0.6 fusion.7.npad
  50.9 0.0 collective-permute-done.5.x3.d0
  50.9 40.0 %up_first.1.sums = f32[4,8,320,512]{3,2,1,0:T(8,128)} custom-call(s32[4,8]{1,0:T(4,128)} %fusion.7.npad, f32[4,2,8,256]{3,2,1,0:T(8,128)} %copy-done, bf16[256,7168]{1,0:T(8,128)(2,1)} %bitcast.25, bf16[256,7168]{1,0:T(8,128)(2,1)} %collective-permute-done.3.x1, bf16[256,3328]{1,0:T(8,128)(2,1)} %collective-permute-done.4.x2.f0, ...), custom_call_target="tpu_custom_call" | custom-call | flops 17448304640 | bytes 109051904 | tf_op jit(solution)/shard_map/up_first/pallas_call | solution.py:259
  90.9 2.5 collective-permute-done.6.f1
  93.4 4.3 %collective-permute-done.7.d1 = bf16[256,3840]{1,0:T(8,128)(2,1)} collective-permute-done((bf16[256,3840]{1,0:T(8,128)(2,1)}, bf16[256,3840]{1,0:T(8,128)(2,1)}, u32[]{:S(2)}, u32[]{:S(2)}) %collective-permute-start.7) | collective-permute-done | bytes 1966112 | tf_op jit(solution)/shard_map/ppermute | solution.py:657
  97.8 130.4 %up_rest.1.h = bf16[8,320,2048]{2,1,0:T(8,128)(2,1)} custom-call(s32[4,8]{1,0:T(4,128)} %fusion.7.npad, f32[4,2,8,256]{3,2,1,0:T(8,128)} %copy-done, bf16[256,7168]{1,0:T(8,128)(2,1)} %bitcast.26, bf16[256,7168]{1,0:T(8,128)(2,1)} %collective-permute-done.3.x1, bf16[256,3328]{1,0:T(8,128)(2,1)} %collective-permute-done.4.x2.f0, ...), custom_call_target="tpu_custom_call" | custom-call | flops 75161927680 | bytes 469762048 | tf_op jit(solution)/shard_map/up_rest/pallas_call | solution.py:281
  228.2 128.1 %down.1 = bf16[256,7168]{1,0:T(8,128)(2,1)} custom-call(f32[4,2,8,256]{3,2,1,0:T(8,128)} %copy-done, bf16[8,320,2048]{2,1,0:T(8,128)(2,1)} %up_rest.1.h, bf16[8,2048,7168]{2,1,0:T(8,128)(2,1)} %wd.1, f32[256,7168]{1,0:T(8,128)} %get-tuple-element.16.shared), custom_call_target="tpu_custom_call" | custom-call | flops 75161927680 | bytes 234881024 | tf_op jit(solution)/shard_map/down/pallas_call | solution.py:622
  356.3 4.1 %copy.12 = bf16[1,1,256,7168]{3,2,1,0:T(8,128)(2,1)} copy(bf16[1,1,256,7168]{3,2,1,0:T(8,128)(2,1)} %bitcast.27) | data formatting | bytes 7340032
  (15 shorter events, 0.1 us)
Async XLA Ops:
  0.0 50.9 %collective-permute-start.3 = (bf16[256,7168]{1,0:T(8,128)(2,1)}, bf16[256,7168]{1,0:T(8,128)(2,1)}, u32[]{:S(2)}, u32[]{:S(2)}) collective-permute-start(bf16[256,7168]{1,0:T(8,128)(2,1)} %bitcast.22), channel_id=1, source_target_pairs={{0,1},{1,0},{2,3},{3,2},{4,5},{5,4},{6,7},{7,6}} | collective-permute-start | bytes 11010056 | tf_op jit(solution)/shard_map/ppermute | solution.py:657
  3.7 40.7 %copy-start.1 = (s32[1,1,256,8]{2,3,1,0:T(8,128)S(1)}, s32[1,1,256,8]{2,3,1,0:T(8,128)}, u32[]{:S(2)}) copy-start(s32[1,1,256,8]{2,3,1,0:T(8,128)} %param.12) | copy-start | bytes 24580
  3.7 40.7 %copy-start.3 = (f32[1,1,256,8]{2,3,1,0:T(8,128)S(1)}, f32[1,1,256,8]{2,3,1,0:T(8,128)}, u32[]{:S(2)}) copy-start(f32[1,1,256,8]{2,3,1,0:T(8,128)} %param.13) | copy-start | bytes 24580
  3.7 40.7 %copy-start.2 = (s32[1,1,256,8]{2,3,1,0:T(8,128)S(1)}, s32[1,1,256,8]{2,3,1,0:T(8,128)}, u32[]{:S(2)}) copy-start(s32[1,1,256,8]{2,3,1,0:T(8,128)} %param.11) | copy-start | bytes 24580
  3.7 40.7 %collective-permute-start.4 = (bf16[256,3328]{1,0:T(8,128)(2,1)}, bf16[256,3328]{1,0:T(8,128)(2,1)}, u32[]{:S(2)}, u32[]{:S(2)}) collective-permute-start(bf16[256,3328]{1,0:T(8,128)(2,1)} %slice.9), channel_id=1, source_target_pairs={{0,2},{1,3},{2,0},{3,1},{4,6},{5,7},{6,4},{7,5}} | collective-permute-start | bytes 5111816 | tf_op jit(solution)/shard_map/ppermute | solution.py:657
  44.3 6.6 %collective-permute-start.5 = (bf16[256,3328]{1,0:T(8,128)(2,1)}, bf16[256,3328]{1,0:T(8,128)(2,1)}, u32[]{:S(2)}, u32[]{:S(2)}) collective-permute-start(bf16[256,3328]{1,0:T(8,128)(2,1)} %collective-permute-done.4.x2.f0), channel_id=1, source_target_pairs={{0,1},{1,0},{2,3},{3,2},{4,5},{5,4},{6,7},{7,6}} | collective-permute-start | bytes 5111816 | tf_op jit(solution)/shard_map/ppermute | solution.py:657
  44.7 3.6 collective-permute-start
  45.2 4.8 %collective-permute-start.1 = (f32[2,8,256]{2,1,0:T(8,128)S(1)}, f32[2,8,256]{2,1,0:T(8,128)S(1)}, u32[]{:S(2)}, u32[]{:S(2)}) collective-permute-start(f32[2,8,256]{2,1,0:T(8,128)S(1)} %get-tuple-element.19), channel_id=1, source_target_pairs={{0,2},{1,3},{2,0},{3,1},{4,6},{5,7},{6,4},{7,5}} | collective-permute-start | bytes 49160 | tf_op jit(solution)/shard_map/ppermute | solution.py:657
  46.9 3.3 collective-permute-start.2
  48.3 45.2 %collective-permute-start.6 = (bf16[256,3840]{1,0:T(8,128)(2,1)}, bf16[256,3840]{1,0:T(8,128)(2,1)}, u32[]{:S(2)}, u32[]{:S(2)}) collective-permute-start(bf16[256,3840]{1,0:T(8,128)(2,1)} %get-tuple-element.13), channel_id=1, source_target_pairs={{0,2},{1,3},{2,0},{3,1},{4,6},{5,7},{6,4},{7,5}} | collective-permute-start | bytes 5898248 | tf_op jit(solution)/shard_map/ppermute | solution.py:657
  50.2 0.7 copy-start
  93.4 4.3 %collective-permute-start.7 = (bf16[256,3840]{1,0:T(8,128)(2,1)}, bf16[256,3840]{1,0:T(8,128)(2,1)}, u32[]{:S(2)}, u32[]{:S(2)}) collective-permute-start(bf16[256,3840]{1,0:T(8,128)(2,1)} %collective-permute-done.6.f1), channel_id=1, source_target_pairs={{0,1},{1,0},{2,3},{3,2},{4,5},{5,4},{6,7},{7,6}} | collective-permute-start | bytes 5898248 | tf_op jit(solution)/shard_map/ppermute | solution.py:657
